TPU v7x, 32 devices: a whole 2x2x4 slice. The times are simulated.
32 devices in a mesh: heads: 4 (over y, core), tokens: 4 (over z), cols: 2 (over x).
Axes of the slice: x: 2, y: 2, z: 4, core: 2. Of those that a mesh axis runs over, the one named last changes fastest.
Arguments:
- query_in: bfloat16 [2048, 8192], P('tokens', ('heads', 'cols')), may hold values from -24 to 24
- key_in: bfloat16 [2048, 8192], P('tokens', ('heads', 'cols')), may hold values from -24 to 24
- value_in: bfloat16 [2048, 8192], P('tokens', ('heads', 'cols')), may hold values from -6 to 6
- out_grads: bfloat16 [2048, 8192], P('tokens', ('heads', 'cols')), may hold values from -6 to 6
- doc_starts: int32 [6], replicated, may hold values from 0 to 2047, as said below
Outputs:
- input_factor: float32 [8192, 8192], P('heads', ('tokens', 'cols'))
- grad_factor: float32 [8192, 8192], P('heads', ('tokens', 'cols'))
Inputs may be any that keep to these rules, and one draw needn't show every extreme that they name: Strictly increasing with the first entry 0; document d runs from doc_starts[d] to the next start (the last one to 2048) - 1. One document holds (4 // 2 + 1) * 512 tokens.
All inputs are finite; a program needn't handle non-finite values.
Results may differ from a plain program's by a relative error of at most 0.0041.
Values may be sent and summed in bfloat16 or wider, within the bound.
A program may use at most 128 MiB of HBM per device.

v0:
```python
import math
import jax
import jax.numpy as jnp
from jax import lax
from jax.sharding import PartitionSpec as P

HEAD_DIM = 128
MASK_FLOOR = -1e30


def spread(value, axis, source):
    kept = jnp.where(lax.axis_index(axis) == source, value, 0).astype(value.dtype)
    return lax.psum(kept, axis)


def document_ids(positions, doc_starts):
    return jnp.sum((positions[:, None] >= doc_starts[None, :]).astype(jnp.int32), axis=1) - 1


def pair_scores(query_rows, key_rows, query_pos, key_pos, doc_starts):
    head_count = query_rows.shape[1] // HEAD_DIM
    query_heads = query_rows.reshape(query_rows.shape[0], head_count, HEAD_DIM)
    key_heads = key_rows.reshape(key_rows.shape[0], head_count, HEAD_DIM)
    scores = jnp.einsum(
        "qhd,khd->hqk", query_heads, key_heads, preferred_element_type=jnp.float32
    ) * (1.0 / math.sqrt(HEAD_DIM))
    query_docs = document_ids(query_pos, doc_starts)
    key_docs = document_ids(key_pos, doc_starts)
    allowed = query_docs[:, None] == key_docs[None, :]
    return (scores, allowed[None, :, :])


def on_device(query_in, key_in, value_in, out_grads, doc_starts):
    tok_dev, row_width = query_in.shape
    head_count = row_width // HEAD_DIM
    first_pos = lax.axis_index("tokens") * tok_dev
    query_pos = first_pos + jnp.arange(tok_dev, dtype=jnp.int32)
    keys_all, values_all = (
        lax.all_gather(key_in, "tokens", axis=0, tiled=True),
        lax.all_gather(value_in, "tokens", axis=0, tiled=True),
    )
    all_tokens = keys_all.shape[0]
    key_span = min(512, all_tokens)
    block_ids = jnp.arange(all_tokens // key_span, dtype=jnp.int32)

    def block_scores(block_id):
        key_begin = block_id * key_span
        key_rows = lax.dynamic_slice_in_dim(keys_all, key_begin, key_span, 0)
        key_pos = key_begin + jnp.arange(key_span, dtype=jnp.int32)
        scores, allowed = pair_scores(query_in, key_rows, query_pos, key_pos, doc_starts)
        return (key_begin, scores, allowed)

    def gated(block_id, update, running):
        key_begin = block_id * key_span
        return update(running)

    def stats_step(running, block_id):

        def update(state):
            row_peak, row_mass = state
            key_begin, scores, allowed = block_scores(block_id)
            masked = jnp.where(allowed, scores, MASK_FLOOR)
            new_peak = jnp.maximum(row_peak, jnp.max(masked, axis=2))
            new_mass = row_mass * jnp.exp(row_peak - new_peak) + jnp.sum(
                jnp.where(allowed, jnp.exp(masked - new_peak[:, :, None]), 0.0), axis=2
            )
            return (new_peak, new_mass)

        return (gated(block_id, update, running), None)

    initial = (
        jnp.full((head_count, tok_dev), MASK_FLOOR, jnp.float32),
        jnp.zeros((head_count, tok_dev), jnp.float32),
    )
    (row_peak, row_mass), _ = lax.scan(stats_step, initial, block_ids)
    log_total = row_peak + jnp.log(row_mass)

    def value_step(running, block_id):

        def update(state):
            weighted, partials = state
            key_begin, scores, allowed = block_scores(block_id)
            weights = jnp.where(allowed, jnp.exp(scores - log_total[:, :, None]), 0.0).astype(
                jnp.bfloat16
            )
            value_rows = lax.dynamic_slice_in_dim(values_all, key_begin, key_span, 0).reshape(
                key_span, head_count, HEAD_DIM
            )
            weighted = weighted + jnp.einsum(
                "hqk,khd->qhd", weights, value_rows, preferred_element_type=jnp.float32
            )
            return (weighted, partials)

        return (gated(block_id, update, running), None)

    partial_rows = 8
    value_init = (
        jnp.zeros((tok_dev, head_count, HEAD_DIM), jnp.float32),
        jnp.zeros((partial_rows, row_width), jnp.float32),
    )
    (weighted, partials), _ = lax.scan(value_step, value_init, block_ids)
    attended = weighted.reshape(tok_dev, row_width).astype(jnp.bfloat16)
    stats_all = lax.all_gather(log_total.T, "tokens", axis=0, tiled=True)
    query_rows = lax.all_gather(query_in, "tokens", axis=0, tiled=True)
    grad_rows = lax.all_gather(out_grads, "tokens", axis=0, tiled=True)
    piece_rows = query_rows.shape[0]
    piece_pos = jnp.arange(piece_rows, dtype=jnp.int32)

    def update(grad_sum):
        scores, allowed = pair_scores(query_rows, key_in, piece_pos, query_pos, doc_starts)
        weights = jnp.where(allowed, jnp.exp(scores - stats_all.T[:, :, None]), 0.0).astype(
            jnp.bfloat16
        )
        piece_grads = grad_rows.reshape(piece_rows, head_count, HEAD_DIM)
        return jnp.einsum("hqk,qhd->khd", weights, piece_grads, preferred_element_type=jnp.float32)

    summed = update(jnp.zeros((tok_dev, head_count, HEAD_DIM), jnp.float32))
    value_grads = summed.reshape(tok_dev, row_width).astype(jnp.bfloat16)
    token_shards = lax.axis_size("tokens")
    col_shards = lax.axis_size("cols")
    rows_attended, rows_grads = (
        lax.all_gather(attended[None], ("tokens", "cols"), axis=0, tiled=True),
        lax.all_gather(value_grads[None], ("tokens", "cols"), axis=0, tiled=True),
    )
    rows_attended = rows_attended.reshape(token_shards, col_shards, tok_dev, row_width)
    rows_grads = rows_grads.reshape(token_shards, col_shards, tok_dev, row_width)
    own_attended = lax.dynamic_index_in_dim(
        rows_attended, lax.axis_index("cols"), 1, keepdims=False
    )
    own_grads = lax.dynamic_index_in_dim(rows_grads, lax.axis_index("cols"), 1, keepdims=False)
    cols_attended, cols_grads = (
        spread(own_attended, "heads", lax.axis_index("tokens")),
        spread(own_grads, "heads", lax.axis_index("tokens")),
    )
    input_factor = jnp.einsum(
        "acnf,ang->cfg", rows_attended, cols_attended, preferred_element_type=jnp.float32
    )
    grad_factor = jnp.einsum(
        "acnf,ang->cfg", rows_grads, cols_grads, preferred_element_type=jnp.float32
    )
    input_factor = input_factor.reshape(col_shards * row_width, row_width) / all_tokens
    grad_factor = grad_factor.reshape(col_shards * row_width, row_width) / all_tokens
    return (input_factor, grad_factor)


def solution(mesh):
    in_specs = (
        P("tokens", ("heads", "cols")),
        P("tokens", ("heads", "cols")),
        P("tokens", ("heads", "cols")),
        P("tokens", ("heads", "cols")),
        P(),
    )
    out_specs = (P("heads", ("tokens", "cols")), P("heads", ("tokens", "cols")))
    return jax.shard_map(
        on_device, mesh=mesh, in_specs=in_specs, out_specs=out_specs, check_vma=False
    )
```

profile of v0, /device:TPU:0, one launch (start us, length us, event | category | flops | bytes accessed | tf_op | source)
XLA Modules:
  0.0 775.8 jit_solution(3249628128545039161)
XLA Ops:
  7.2 2.4 copy.58
  9.7 2.3 copy.57
  12.8 2.3 copy.62
  15.1 78.1 %all-gather.9.cloned.1.call-done = bf16[2048,1024]{0,1:T(8,128)(2,1)} async-done(((bf16[512,1024]{0,1:T(8,128)(2,1)}), bf16[2048,1024]{0,1:T(8,128)(2,1)}) %all-gather.9.cloned.1.call-update) | async-done | bytes 4194320 | tf_op jit(solution)/shard_map/all_gather | solution.py:39
  93.2 27.0 %while.30 = (s32[]{:T(128)}, f32[8,512]{1,0:T(8,128)S(1)}, f32[8,512]{1,0:T(8,128)S(1)}, s32[6]{0:T(128)S(1)}, s32[4]{0:T(128)S(1)}, /*index=5*/bf16[2048,1024]{...) while((s32[]{:T(128)}, f32[8,512]{1,0:T(8,128)S(1)}, ...), condition=%wide.region_5.6_spmd.clone, body=%wide.region_0.5_spmd.clone.sunk | while | flops 553950208 | bytes 21995748 | solution.py:75
  96.1 1.7 fusion.59
  97.9 2.0 select_reduce_fusion.2
  104.7 2.0 select_reduce_fusion.2
  111.4 2.0 select_reduce_fusion.2
  118.2 2.0 select_reduce_fusion.2
  120.3 54.3 %all-gather.7.cloned.1.call-done = bf16[2048,1024]{0,1:T(8,128)(2,1)} async-done(((bf16[512,1024]{0,1:T(8,128)(2,1)}), bf16[2048,1024]{0,1:T(8,128)(2,1)}) %all-gather.7.cloned.1.call-update) | async-done | bytes 4194320 | tf_op jit(solution)/shard_map/all_gather | solution.py:40
  174.6 34.2 %while.31 = (s32[]{:T(128)}, f32[512,8,128]{0,2,1:T(8,128)}, s32[4]{0:T(128)S(1)}, bf16[2048,1024]{0,1:T(8,128)(2,1)}, s32[6]{0:T(128)S(1)}, /*index=5*/bf16[204...) while((s32[]{:T(128)}, f32[512,8,128]{0,2,1:T(8,128)}, ...), condition=%wide.region_9.10_spmd.clone, body=%wide.region_6.9_spmd.clone.sunk | while | flops 1083460608 | bytes 12099821 | solution.py:101
  177.9 4.0 bitcast_add_fusion.2
  183.5 1.9 constant_dynamic-slice_fusion.6
  185.4 5.6 bitcast_add_fusion.2
  194.3 5.6 bitcast_add_fusion.2
  203.2 5.6 bitcast_add_fusion.2
  208.8 1.8 convert_element_type.76
  213.0 42.4 %all-gather.15.cloned.1.call-done = bf16[2048,1024]{1,0:T(8,128)(2,1)} async-done(((bf16[512,1024]{1,0:T(8,128)(2,1)}), bf16[2048,1024]{1,0:T(8,128)(2,1)}) %all-gather.15.cloned.1.call-update) | async-done | bytes 4194320 | tf_op jit(solution)/shard_map/all_gather | solution.py:105
  255.5 6.4 copy.65
  261.9 15.2 %all_gather.25 = f32[2048,8]{0,1:T(8,128)S(1)} all-gather(f32[512,8]{0,1:T(8,128)S(1)} %bitcast.132), channel_id=1, replica_groups=mesh['heads'=4,'tokens'=4,'cols'=2] {'tokens'}, dimensions={0}, use_global_device_ids=true | all-gather | bytes 81920 | tf_op jit(solution)/shard_map/all_gather | solution.py:103
  277.1 59.8 %all-gather.13.cloned.1.call-done = bf16[2048,1024]{0,1:T(8,128)(2,1)} async-done(((bf16[512,1024]{0,1:T(8,128)(2,1)}), bf16[2048,1024]{0,1:T(8,128)(2,1)}) %all-gather.13.cloned.1.call-update) | async-done | bytes 4194320 | tf_op jit(solution)/shard_map/all_gather | solution.py:104
  336.9 14.4 %fusion.29 = bf16[8,512,128]{1,2,0:T(8,128)(2,1)S(1)} fusion(bf16[2048,8,128]{0,2,1:T(8,128)(2,1)} %bitcast.130, bf16[2048,8,128]{0,2,1:T(8,128)(2,1)} %bitcast.134, f32[8,2048]{1,0:T(8,128)S(1)} %bitcast.133, pred[2048,512]{1,0:T(8,128)(4,1)S(1)} %broadcast_compare_fusion.2, bf16[512,1024]{1,0:T(8,128)(2,1)S(1)} %copy-done.2), kind=kOutput, calls=%fused_computation.50 | convolution fusion | flops 4329046016 | bytes 11599872 | tf_op jit(solution)/shard_map/hqk,qhd->khd/dot_general | solution.py:115
  353.0 109.4 %all-gather.11.cloned.1.call-done = bf16[8,512,1024]{2,1,0:T(8,128)(2,1)} async-done(((bf16[1,512,1024]{2,1,0:T(8,128)(2,1)}), bf16[8,512,1024]{2,1,0:T(8,128)(2,1)}) %all-gather.11.cloned.1.call-update) | async-done | bytes 8388624 | tf_op jit(solution)/shard_map/all_gather | solution.py:122
  462.4 4.5 fusion.27
  466.9 120.8 %all-gather.17.cloned.1.call-done = bf16[8,512,1024]{2,1,0:T(8,128)(2,1)} async-done(((bf16[1,512,1024]{2,1,0:T(8,128)(2,1)}), bf16[8,512,1024]{2,1,0:T(8,128)(2,1)}) %all-gather.17.cloned.1.call-update) | async-done | bytes 8388624 | tf_op jit(solution)/shard_map/all_gather | solution.py:123
  587.6 4.4 fusion.26
  592.1 11.5 %copy.60 = bf16[2,1024,4,512]{3,1,0,2:T(8,128)(2,1)} copy(bf16[2,1024,4,512]{1,3,0,2:T(8,128)(2,1)} %bitcast.124) | data formatting | bytes 16777216 | tf_op jit(solution)/shard_map/acnf,ang->cfg/dot_general | solution.py:135
  603.6 11.5 %copy.67 = bf16[2,1024,4,512]{3,1,0,2:T(8,128)(2,1)} copy(bf16[2,1024,4,512]{1,3,0,2:T(8,128)(2,1)} %bitcast.126) | data formatting | bytes 16777216 | tf_op jit(solution)/shard_map/acnf,ang->cfg/dot_general | solution.py:138
  615.1 128.2 %all-reduce.3.cloned.1.call-done = (bf16[4,512,1024]{2,1,0:T(8,128)(2,1)}, bf16[4,512,1024]{2,1,0:T(8,128)(2,1)}) async-done(((bf16[4,512,1024]{2,1,0:T(8,128)(2,1)}, bf16[4,512,1024]{2,1,0:T(8,128)(2,1)}), (bf16[4,512,1024]{2,1,0:T(8,128)(2,1)}, bf16[4,512,1024]{2,1,0:T(8,128)(2,1)})) %all-reduce.3.cloned.1.call-update) | async-done | bytes 8388624 | tf_op jit(solution)/shard_map/psum | solution.py:13
  743.3 14.6 %bitcast_multiply_fusion.1 = f32[2048,1024]{1,0:T(8,128)} fusion(bf16[2048,4,512]{2,0,1:T(8,128)(2,1)} %bitcast.128, bf16[4,512,1024]{2,1,0:T(8,128)(2,1)} %get-tuple-element.383), kind=kOutput, calls=%fused_computation.43 | convolution fusion | flops 8592031744 | bytes 20971520 | tf_op jit(solution)/shard_map/acnf,ang->cfg/dot_general | solution.py:135
  757.9 11.0 %bitcast_multiply_fusion = f32[2048,1024]{1,0:T(8,128)} fusion(bf16[2048,4,512]{2,0,1:T(8,128)(2,1)S(1)} %bitcast.127, bf16[4,512,1024]{2,1,0:T(8,128)(2,1)S(1)} %copy-done.4), kind=kOutput, calls=%fused_computation.42 | convolution fusion | flops 8592031744 | bytes 20971520 | tf_op jit(solution)/shard_map/acnf,ang->cfg/dot_general | solution.py:138
  (108 shorter events, 27.9 us)
Async XLA Ops:
  7.2 86.1 %copy-start = (bf16[512,1024]{1,0:T(8,128)(2,1)S(1)}, bf16[512,1024]{1,0:T(8,128)(2,1)}, u32[]{:S(2)}) copy-start(bf16[512,1024]{1,0:T(8,128)(2,1)} %param.9) | copy-start | bytes 3145732
  7.2 86.1 %copy-start.3 = (s32[6]{0:T(128)S(1)}, s32[6]{0:T(128)}, u32[]{:S(2)}) copy-start(s32[6]{0:T(128)} %param.13) | copy-start | bytes 76
  7.2 86.0 %all-gather.9.cloned.1.call-start = ((), (), s32[]{:S(2)}) async-start(), calls=%async_computation.1 | async-start | bytes 5242880 | tf_op jit(solution)/shard_map/all_gather | solution.py:39
  9.6 165.0 %all-gather.7.cloned.1.call-start = ((), (), s32[]{:S(2)}) async-start(), calls=%async_computation | async-start | bytes 5242880 | tf_op jit(solution)/shard_map/all_gather | solution.py:40
  12.0 243.5 %all-gather.15.cloned.1.call-start = ((), (), s32[]{:S(2)}) async-start(), calls=%async_computation.4 | async-start | bytes 5242880 | tf_op jit(solution)/shard_map/all_gather | solution.py:105
  12.7 324.2 %all-gather.13.cloned.1.call-start = ((), (), s32[]{:S(2)}) async-start(), calls=%async_computation.3 | async-start | bytes 5242880 | tf_op jit(solution)/shard_map/all_gather | solution.py:104
  15.0 447.3 %all-gather.11.cloned.1.call-start = ((), (), s32[]{:S(2)}) async-start(), calls=%async_computation.2 | async-start | bytes 9437184 | tf_op jit(solution)/shard_map/all_gather | solution.py:122
  208.8 128.1 %copy-start.2 = (bf16[512,1024]{1,0:T(8,128)(2,1)S(1)}, bf16[512,1024]{1,0:T(8,128)(2,1)}, u32[]{:S(2)}) copy-start(bf16[512,1024]{1,0:T(8,128)(2,1)} %param.10) | copy-start | bytes 3145732
  212.0 375.6 %all-gather.17.cloned.1.call-start = ((), (), s32[]{:S(2)}) async-start(), calls=%async_computation.5 | async-start | bytes 9437184 | tf_op jit(solution)/shard_map/all_gather | solution.py:123
  352.7 390.6 %all-reduce.3.cloned.1.call-start = ((), (), s32[]{:S(2)}) async-start(), calls=%async_computation.6 | async-start | bytes 16777216 | tf_op jit(solution)/shard_map/psum | solution.py:13
  743.3 14.6 %copy-start.1 = (bf16[2,1024,4,512]{3,1,0,2:T(8,128)(2,1)S(1)}, bf16[2,1024,4,512]{3,1,0,2:T(8,128)(2,1)}, u32[]{:S(2)}) copy-start(bf16[2,1024,4,512]{3,1,0,2:T(8,128)(2,1)} %copy.67) | copy-start | bytes 25165828
  743.3 14.6 %copy-start.4 = (bf16[4,512,1024]{2,1,0:T(8,128)(2,1)S(1)}, bf16[4,512,1024]{2,1,0:T(8,128)(2,1)}, u32[]{:S(2)}) copy-start(bf16[4,512,1024]{2,1,0:T(8,128)(2,1)} %get-tuple-element.384) | copy-start | bytes 12582916
Sparse Core Ops, SparseCore 0:
  9.7 83.4 all-gather.8
  95.4 79.2 all-gather.6
  176.2 79.2 all-gather.14
  256.9 79.9 all-gather.12
  339.5 122.8 all-gather.10
  464.9 122.6 all-gather.16
  592.2 151.0 all-reduce.2
where the time goes:
time: 777 us; the launch traced here: 776 us
  waiting for transfers between devices  594 us (76%)
  matrix products  67.8 us (9%)
  local copies, waits for them, and re-layouts  56 us (7%)
  other arithmetic  22.4 us (3%)
  blocking collectives  15.2 us (2%)
  between operations  14.2 us (2%)
    psum x1, waiting for transfers between devices, spread(): return lax.psum(kept, axis)  128 us
    all_gather x1, waiting for transfers between devices, on_device(): lax.all_gather(value_grads[None], ('tokens', 'cols'), axis=0, tiled=True)  121 us
    all_gather x1, waiting for transfers between devices, on_device(): lax.all_gather(attended[None], ('tokens', 'cols'), axis=0, tiled=True)  109 us
    all_gather x1, waiting for transfers between devices, on_device(): lax.all_gather(key_in, 'tokens', axis=0, tiled=True)  78.1 us
    all_gather x1, waiting for transfers between devices, on_device(): query_rows = lax.all_gather(query_in, 'tokens', axis=0, tiled=True)  59.8 us
    all_gather x1, waiting for transfers between devices, on_device(): lax.all_gather(value_in, 'tokens', axis=0, tiled=True)  54.3 us
    all_gather x1, waiting for transfers between devices, on_device(): grad_rows = lax.all_gather(out_grads, 'tokens', axis=0, tiled=True)  42.4 us
    dot_general x4, matrix products, update(): jnp.einsum('hqk,khd->qhd', weights, value_rows, preferred_element_type=jn...  20.8 us
  transfers between devices with their start and end apart: 7, of which 7 were waited for; matrix products, arithmetic and copies ran while one was open for 15% of the time, Pallas kernels for 0%

commit v1 on v0

--- a/solution.py
+++ b/solution.py
@@ -10,7 +10,8 @@
 
 def spread(value, axis, source):
     kept = jnp.where(lax.axis_index(axis) == source, value, 0).astype(value.dtype)
-    return lax.psum(kept, axis)
+    routes_all_edit = lambda a0, along_axis: jnp.sum(lax.all_gather(a0, along_axis), 0)
+    return routes_all_edit(kept, axis)
 
 
 def document_ids(positions, doc_starts):

time: 777 us -> 845 us (1.088)
  other arithmetic: 22.4 us -> 56.6 us
  waiting for transfers between devices: 594 us -> 615 us
  matrix products: 67.8 us -> 80.2 us
    all_gather x0 -> x2, waiting for transfers between devices: none -> 173 us  [spread(): lax.all_gather(a0, along_axis)]
    psum x1 -> x0, waiting for transfers between devices: 128 us -> none  [spread(): return lax.psum(kept, axis)]
    all_gather x1, waiting for transfers between devices: 54.3 us -> 30.1 us  [on_device(): lax.all_gather(value_in, 'tokens', axis=0, tiled=True)]
    unnamed x3 -> x6, other arithmetic: 0.01 us -> 23.9 us
    dot_general x4, matrix products: 6.96 us -> 20.6 us  [pair_scores(): jnp.einsum('qhd,khd->hqk', query_heads, key_heads, preferred_element_type...]
    reduce_sum x4, other arithmetic: 8.14 us -> 18.3 us  [update(): jnp.sum(jnp.where(allowed, jnp.exp(masked - new_peak[:, :, None]), 0.0),...]
  transfers between devices with their start and end apart: 7 -> 8, of which waited for: 7 -> 8; matrix products, arithmetic and copies ran while one was open for 15% -> 18% of each run, Pallas kernels for 0% -> 0%
where the time goes in v1:
time: 845 us; the launch traced here: 843 us
  waiting for transfers between devices  615 us (73%)
  matrix products  80.2 us (9%)
  other arithmetic  56.6 us (7%)
  local copies, waits for them, and re-layouts  56.4 us (7%)
  blocking collectives  15.2 us (2%)
  between operations  14.3 us (2%)
    all_gather x2, waiting for transfers between devices, spread(): lax.all_gather(a0, along_axis)  173 us
    all_gather x1, waiting for transfers between devices, on_device(): lax.all_gather(value_grads[None], ('tokens', 'cols'), axis=0, tiled=True)  120 us
    all_gather x1, waiting for transfers between devices, on_device(): lax.all_gather(attended[None], ('tokens', 'cols'), axis=0, tiled=True)  110 us
    all_gather x1, waiting for transfers between devices, on_device(): lax.all_gather(key_in, 'tokens', axis=0, tiled=True)  78.5 us
    all_gather x1, waiting for transfers between devices, on_device(): query_rows = lax.all_gather(query_in, 'tokens', axis=0, tiled=True)  59.8 us
    all_gather x1, waiting for transfers between devices, on_device(): grad_rows = lax.all_gather(out_grads, 'tokens', axis=0, tiled=True)  42.4 us
    all_gather x1, waiting for transfers between devices, on_device(): lax.all_gather(value_in, 'tokens', axis=0, tiled=True)  30.1 us
    unnamed x6, other arithmetic  23.9 us
  transfers between devices with their start and end apart: 8, of which 8 were waited for; matrix products, arithmetic and copies ran while one was open for 18% of the time, Pallas kernels for 0%

profile of v1, /device:TPU:0, one launch (start us, length us, event | category | flops | bytes accessed | tf_op | source)
XLA Modules:
  0.0 843.5 jit_solution(14831967319808678650)
XLA Ops:
  15.1 78.5 %all-gather.13.cloned.1.call-done = bf16[2048,1024]{0,1:T(8,128)(2,1)} async-done(((bf16[512,1024]{0,1:T(8,128)(2,1)}), bf16[2048,1024]{0,1:T(8,128)(2,1)}) %all-gather.13.cloned.1.call-update) | async-done | bytes 4194320 | tf_op jit(solution)/shard_map/all_gather | solution.py:40
  93.6 50.7 %while.30 = (s32[]{:T(128)}, f32[8,512]{1,0:T(8,128)S(1)}, f32[8,512]{1,0:T(8,128)S(1)}, s32[6]{0:T(128)S(1)}, s32[4]{0:T(128)S(1)}, /*index=5*/bf16[2048,1024]{...) while((s32[]{:T(128)}, f32[8,512]{1,0:T(8,128)S(1)}, ...), condition=%wide.region_5.6_spmd.clone, body=%wide.region_0.5_spmd.clone.sunk | while | flops 553950208 | bytes 21995740 | solution.py:76
  96.5 5.2 fusion.57
  101.7 4.9 select_reduce_fusion.2
  109.5 5.1 fusion.57
  114.7 4.5 select_reduce_fusion.2
  122.1 5.1 fusion.57
  127.3 4.5 select_reduce_fusion.2
  134.7 5.1 fusion.57
  139.8 4.5 select_reduce_fusion.2
  144.4 30.1 %all-gather.11.cloned.1.call-done = bf16[2048,1024]{0,1:T(8,128)(2,1)} async-done(((bf16[512,1024]{0,1:T(8,128)(2,1)}), bf16[2048,1024]{0,1:T(8,128)(2,1)}) %all-gather.11.cloned.1.call-update) | async-done | bytes 4194320 | tf_op jit(solution)/shard_map/all_gather | solution.py:41
  174.5 34.2 %while.31 = (s32[]{:T(128)}, f32[512,8,128]{0,2,1:T(8,128)}, s32[4]{0:T(128)S(1)}, bf16[2048,1024]{0,1:T(8,128)(2,1)}, s32[6]{0:T(128)S(1)}, /*index=5*/bf16[204...) while((s32[]{:T(128)}, f32[512,8,128]{0,2,1:T(8,128)}, ...), condition=%wide.region_9.10_spmd.clone, body=%wide.region_6.9_spmd.clone.sunk | while | flops 1083460608 | bytes 12099813 | solution.py:102
  185.3 5.6 bitcast_add_fusion.2
  194.2 5.6 bitcast_add_fusion.2
  203.1 5.6 bitcast_add_fusion.2
  212.9 42.4 %all-gather.19.cloned.1.call-done = bf16[2048,1024]{1,0:T(8,128)(2,1)} async-done(((bf16[512,1024]{1,0:T(8,128)(2,1)}), bf16[2048,1024]{1,0:T(8,128)(2,1)}) %all-gather.19.cloned.1.call-update) | async-done | bytes 4194320 | tf_op jit(solution)/shard_map/all_gather | solution.py:106
  255.3 6.4 copy.64
  261.7 15.2 %all_gather.34 = f32[2048,8]{0,1:T(8,128)S(1)} all-gather(f32[512,8]{0,1:T(8,128)S(1)} %bitcast.130), channel_id=1, replica_groups=mesh['heads'=4,'tokens'=4,'cols'=2] {'tokens'}, dimensions={0}, use_global_device_ids=true | all-gather | bytes 81920 | tf_op jit(solution)/shard_map/all_gather | solution.py:104
  277.0 59.8 %all-gather.17.cloned.1.call-done = bf16[2048,1024]{0,1:T(8,128)(2,1)} async-done(((bf16[512,1024]{0,1:T(8,128)(2,1)}), bf16[2048,1024]{0,1:T(8,128)(2,1)}) %all-gather.17.cloned.1.call-update) | async-done | bytes 4194320 | tf_op jit(solution)/shard_map/all_gather | solution.py:105
  336.8 14.4 %fusion.27 = bf16[8,512,128]{1,2,0:T(8,128)(2,1)S(1)} fusion(bf16[2048,8,128]{0,2,1:T(8,128)(2,1)} %bitcast.128, bf16[2048,8,128]{0,2,1:T(8,128)(2,1)} %bitcast.132, f32[8,2048]{1,0:T(8,128)S(1)} %bitcast.131, pred[2048,512]{1,0:T(8,128)(4,1)S(1)} %broadcast_compare_fusion.2, bf16[512,1024]{1,0:T(8,128)(2,1)S(1)} %copy-done.2), kind=kOutput, calls=%fused_computation.50 | convolution fusion | flops 4329046016 | bytes 11599872 | tf_op jit(solution)/shard_map/hqk,qhd->khd/dot_general | solution.py:116
  352.6 109.7 %all-gather.15.cloned.1.call-done = bf16[8,512,1024]{2,1,0:T(8,128)(2,1)} async-done(((bf16[1,512,1024]{2,1,0:T(8,128)(2,1)}), bf16[8,512,1024]{2,1,0:T(8,128)(2,1)}) %all-gather.15.cloned.1.call-update) | async-done | bytes 8388624 | tf_op jit(solution)/shard_map/all_gather | solution.py:123
  462.2 4.5 dynamic-slice_select_fusion.1
  467.0 120.5 %all-gather.21.cloned.1.call-done = bf16[8,512,1024]{2,1,0:T(8,128)(2,1)} async-done(((bf16[1,512,1024]{2,1,0:T(8,128)(2,1)}), bf16[8,512,1024]{2,1,0:T(8,128)(2,1)}) %all-gather.21.cloned.1.call-update) | async-done | bytes 8388624 | tf_op jit(solution)/shard_map/all_gather | solution.py:124
  587.5 4.5 dynamic-slice_select_fusion
  592.0 12.0 %copy.58 = bf16[2,1024,4,512]{3,1,0,2:T(8,128)(2,1)} copy(bf16[2,1024,4,512]{1,3,0,2:T(8,128)(2,1)} %bitcast.118) | data formatting | bytes 16777216 | tf_op jit(solution)/shard_map/acnf,ang->cfg/dot_general | solution.py:136
  604.0 11.5 %copy.66 = bf16[2,1024,4,512]{3,1,0,2:T(8,128)(2,1)} copy(bf16[2,1024,4,512]{1,3,0,2:T(8,128)(2,1)} %bitcast.120) | data formatting | bytes 16777216 | tf_op jit(solution)/shard_map/acnf,ang->cfg/dot_general | solution.py:139
  615.6 78.2 %all-gather.23.cloned.1.call-done = bf16[16,1,512,1024]{3,2,1,0:T(8,128)(2,1)} async-done(((bf16[4,1,512,1024]{3,2,1,0:T(8,128)(2,1)}), bf16[16,1,512,1024]{3,2,1,0:T(8,128)(2,1)}) %all-gather.23.cloned.1.call-update) | async-done | bytes 16777232 | tf_op jit(solution)/shard_map/all_gather | solution.py:13
  693.7 12.8 %bitcast_reduce_fusion.1 = bf16[4,512,1024]{2,1,0:T(8,128)(2,1)} fusion(bf16[4,4,512,1024]{3,2,1,0:T(8,128)(2,1)} %bitcast.121), kind=kLoop, calls=%fused_computation.43 | loop fusion | flops 6291456 | bytes 20971520
  706.5 94.7 %all-gather.25.cloned.1.call-done = bf16[16,1,512,1024]{3,2,1,0:T(8,128)(2,1)} async-done(((bf16[4,1,512,1024]{3,2,1,0:T(8,128)(2,1)}), bf16[16,1,512,1024]{3,2,1,0:T(8,128)(2,1)}) %all-gather.25.cloned.1.call-update) | async-done | bytes 16777232 | tf_op jit(solution)/shard_map/all_gather | solution.py:13
  801.2 11.0 %bitcast_reduce_fusion = bf16[4,512,1024]{2,1,0:T(8,128)(2,1)S(1)} fusion(bf16[4,4,512,1024]{3,2,1,0:T(8,128)(2,1)} %bitcast.122), kind=kLoop, calls=%fused_computation.42 | loop fusion | flops 6291456 | bytes 20971520
  812.3 13.4 %bitcast_multiply_fusion.1 = f32[2048,1024]{1,0:T(8,128)} fusion(bf16[2048,4,512]{2,0,1:T(8,128)(2,1)} %bitcast.126, bf16[4,512,1024]{2,1,0:T(8,128)(2,1)S(1)} %copy-done.1), kind=kOutput, calls=%fused_computation.45 | convolution fusion | flops 8592031744 | bytes 20971520 | tf_op jit(solution)/shard_map/acnf,ang->cfg/dot_general | solution.py:136
  825.6 11.0 %bitcast_multiply_fusion = f32[2048,1024]{1,0:T(8,128)} fusion(bf16[2048,4,512]{2,0,1:T(8,128)(2,1)S(1)} %bitcast.125, bf16[4,512,1024]{2,1,0:T(8,128)(2,1)S(1)} %bitcast_reduce_fusion), kind=kOutput, calls=%fused_computation.44 | convolution fusion | flops 8592031744 | bytes 20971520 | tf_op jit(solution)/shard_map/acnf,ang->cfg/dot_general | solution.py:139
  (116 shorter events, 37.2 us)
Async XLA Ops:
  7.2 86.5 %copy-start = (bf16[512,1024]{1,0:T(8,128)(2,1)S(1)}, bf16[512,1024]{1,0:T(8,128)(2,1)}, u32[]{:S(2)}) copy-start(bf16[512,1024]{1,0:T(8,128)(2,1)} %param.9) | copy-start | bytes 3145732
  7.2 86.5 %copy-start.3 = (s32[6]{0:T(128)S(1)}, s32[6]{0:T(128)}, u32[]{:S(2)}) copy-start(s32[6]{0:T(128)} %param.13) | copy-start | bytes 76
  7.2 86.4 %all-gather.13.cloned.1.call-start = ((), (), s32[]{:S(2)}) async-start(), calls=%async_computation.1 | async-start | bytes 5242880 | tf_op jit(solution)/shard_map/all_gather | solution.py:40
  9.6 164.8 %all-gather.11.cloned.1.call-start = ((), (), s32[]{:S(2)}) async-start(), calls=%async_computation | async-start | bytes 5242880 | tf_op jit(solution)/shard_map/all_gather | solution.py:41
  12.0 243.3 %all-gather.19.cloned.1.call-start = ((), (), s32[]{:S(2)}) async-start(), calls=%async_computation.4 | async-start | bytes 5242880 | tf_op jit(solution)/shard_map/all_gather | solution.py:106
  12.7 324.1 %all-gather.17.cloned.1.call-start = ((), (), s32[]{:S(2)}) async-start(), calls=%async_computation.3 | async-start | bytes 5242880 | tf_op jit(solution)/shard_map/all_gather | solution.py:105
  15.0 447.2 %all-gather.15.cloned.1.call-start = ((), (), s32[]{:S(2)}) async-start(), calls=%async_computation.2 | async-start | bytes 9437184 | tf_op jit(solution)/shard_map/all_gather | solution.py:123
  208.7 128.1 %copy-start.2 = (bf16[512,1024]{1,0:T(8,128)(2,1)S(1)}, bf16[512,1024]{1,0:T(8,128)(2,1)}, u32[]{:S(2)}) copy-start(bf16[512,1024]{1,0:T(8,128)(2,1)} %param.10) | copy-start | bytes 3145732
  211.9 375.6 %all-gather.21.cloned.1.call-start = ((), (), s32[]{:S(2)}) async-start(), calls=%async_computation.5 | async-start | bytes 9437184 | tf_op jit(solution)/shard_map/all_gather | solution.py:124
  352.5 341.2 %all-gather.23.cloned.1.call-start = ((), (), s32[]{:S(2)}) async-start(), calls=%async_computation.6 | async-start | bytes 20971520 | tf_op jit(solution)/shard_map/all_gather | solution.py:13
  466.7 334.5 %all-gather.25.cloned.1.call-start = ((), (), s32[]{:S(2)}) async-start(), calls=%async_computation.7 | async-start | bytes 20971520 | tf_op jit(solution)/shard_map/all_gather | solution.py:13
  801.2 11.0 %copy-start.1 = (bf16[4,512,1024]{2,1,0:T(8,128)(2,1)S(1)}, bf16[4,512,1024]{2,1,0:T(8,128)(2,1)}, u32[]{:S(2)}) copy-start(bf16[4,512,1024]{2,1,0:T(8,128)(2,1)} %bitcast_reduce_fusion.1) | copy-start | bytes 12582916
  801.2 24.4 %slice-start = ((s8[8388608]{0:T(1024)(128)(4,1)}), s8[4194304]{0:T(1024)(128)(4,1)S(1)}, s32[]{:S(2)}) async-start(s8[8388608]{0:T(1024)(128)(4,1)} %bitcast.123), calls=%async_computation.8 | async-start | bytes 8388608
  812.2 13.4 %slice-start.1 = ((s8[8388608]{0:T(1024)(128)(4,1)}), s8[4194304]{0:T(1024)(128)(4,1)S(1)}, s32[]{:S(2)}) async-start(s8[8388608]{0:T(1024)(128)(4,1)} %bitcast.123), calls=%async_computation.9 | async-start | bytes 8388608
Sparse Core Ops, SparseCore 0:
  10.1 83.4 all-gather.12
  95.2 79.2 all-gather.10
  176.0 79.2 all-gather.18
  256.7 79.9 all-gather.16
  339.3 122.8 all-gather.14
  464.8 122.6 all-gather.20
  589.6 104.0 all-gather.22
  695.3 105.8 all-gather.24
